TPU v7x, 32 devices: a whole 2x2x4 slice. The times are simulated.
32 devices in a mesh: coil: 4 (over y, core), spoke: 8 (over z, x).
Axes of the slice: x: 2, y: 2, z: 4, core: 2. Of those that a mesh axis runs over, the one named last changes fastest.
Arguments:
- kdata: bfloat16 [64, 8, 2, 64, 256], P('spoke', 'coil'), may hold values from -6 to 6
- coords: float32 [64, 2, 256], P('spoke'), may hold values from 0 to 256, as said below
- foot_offset: int32 [64, 8], P('spoke'), may hold values from 0 to 224, as said below
- live_count: int32 [8], P('spoke'), may hold values from 1 to 8, 48 in all
- dcf_table: float32 [129], replicated, may hold values from 0.1 to 4
- dcf_index: int32 [64, 256], P('spoke'), may hold values from 0 to 128
- slab_owner: int32 [8], replicated, may hold values from 0 to 7, each once
Outputs:
- coil_images: float32 [256, 8, 2, 64, 256], P('spoke', 'coil')
- combined: float32 [256, 64, 256], P('spoke', 'coil')
Inputs may be any that keep to these rules, and one draw needn't show every extreme that they name: coords[p, 0, s] lies between s and s + 1; coords[p, 1, s] lies between foot_offset[p, s // 32] + 3 and foot_offset[p, s // 32] + 29. `foot_offset`: for each block of 8 spoke slots (the slots of one device index of spoke) and each slab, the offsets lie between b and b + 16, where b is the smallest of them, and both ends are taken; b <= 208.
All inputs are finite; a program needn't handle non-finite values. No bound on the sum of `live_count` on one device may be relied on, other than what follows from the above.
Results may differ from a plain program's by a relative error of at most 0.0028.
Values may be sent and summed in bfloat16 or wider, within the bound.
A program may use at most 128 MiB of HBM per device.

v0:
```python
import math

import jax
import jax.numpy as jnp
from jax import lax
from jax.sharding import PartitionSpec as P

FW = 32
UW = 48
HALO = 4


def kernel(distance):
    inner = jnp.maximum(1.0 - distance * distance * 0.25, 0.0)
    return inner * inner


def inverse_table(length):
    counter = jnp.arange(length, dtype=jnp.int32)
    phase = (
        2.0 * math.pi / length * (counter[:, None] * counter[None, :] % length).astype(jnp.float32)
    )
    factor = 1.0 / math.sqrt(length)
    return (jnp.cos(phase) * factor, jnp.sin(phase) * factor)


def product(left, right):
    return jnp.dot(left, right, precision=lax.Precision.HIGHEST, preferred_element_type=jnp.float32)


def depth_product(left, right):
    return jnp.einsum("akg,kz->azg", left, right, precision=lax.Precision.HIGHEST)


def on_device(kdata, coords, foot_offset, live_count, dcf_table, dcf_index, slab_owner):
    slot_count, coil_dev, part_count, kz_len, grid_len = kdata.shape
    slab_count = lax.axis_size("spoke")
    slab_rows = grid_len // slab_count
    block_len = slab_rows + 2 * HALO
    columns = coil_dev * part_count * kz_len
    live_flag = (jnp.arange(slot_count, dtype=jnp.int32) < live_count[0]).astype(jnp.float32)
    table_len = dcf_table.shape[0]
    table_hit = dcf_index[:, :, None] == jnp.arange(table_len, dtype=jnp.int32)[None, None, :]
    density = (
        jnp.sum(jnp.where(table_hit, dcf_table[None, None, :], 0.0), axis=2) * live_flag[:, None]
    )
    slab_first = jnp.arange(slab_count, dtype=jnp.int32) * slab_rows
    position = (
        slab_first[:, None] - HALO + jnp.arange(block_len, dtype=jnp.int32)[None, :]
    ).reshape(-1)
    inside = ((position >= 0) & (position < grid_len)).reshape(slab_count, block_len)
    clipped = jnp.clip(position, 0, grid_len - 1)
    samples_last = jnp.transpose(kdata.reshape(slot_count, columns, grid_len), (0, 2, 1))
    blocks = jnp.take(samples_last, clipped, axis=1).reshape(
        slot_count, slab_count, block_len, columns
    )
    blocks = jnp.where(inside[None, :, :, None], blocks, jnp.zeros((), kdata.dtype))
    row_coord = jnp.take(coords[:, 0, :], clipped, axis=1).reshape(
        slot_count, slab_count, block_len
    )
    col_coord = jnp.take(coords[:, 1, :], clipped, axis=1).reshape(
        slot_count, slab_count, block_len
    )
    block_density = jnp.where(
        inside[None],
        jnp.take(density, clipped, axis=1).reshape(slot_count, slab_count, block_len),
        0.0,
    )
    device = lax.axis_index("spoke")
    owned_slab = slab_owner[device]
    start_cols = jnp.broadcast_to(
        foot_offset.astype(jnp.float32)[:, :, None], (slot_count, slab_count, block_len)
    )
    geometry = jnp.stack([row_coord, col_coord, block_density, start_cols], axis=2)
    sent_values = jnp.take(blocks, slab_owner, axis=1)
    sent_geometry = jnp.take(geometry, slab_owner, axis=1)
    got_values = lax.all_to_all(
        sent_values, "spoke", split_axis=1, concat_axis=0, tiled=True
    ).reshape(slab_count, slot_count, block_len, columns)
    got_geometry = lax.all_to_all(
        sent_geometry, "spoke", split_axis=1, concat_axis=0, tiled=True
    ).reshape(slab_count, slot_count, 4, block_len)
    row_cells = (owned_slab * slab_rows + jnp.arange(slab_rows, dtype=jnp.int32)).astype(
        jnp.float32
    )
    window_cols = jnp.arange(UW, dtype=jnp.int32)
    grid_cols = jnp.arange(grid_len, dtype=jnp.int32)
    senders = min(8, slab_count)

    def add_block(turn_index, running):
        values = lax.dynamic_slice_in_dim(got_values, turn_index * senders, senders, 0)
        geometry_part = lax.dynamic_slice_in_dim(got_geometry, turn_index * senders, senders, 0)
        sender_base = jnp.min(geometry_part[:, :, 3, 0], axis=1).astype(jnp.int32)
        cells = (sender_base[:, None] + window_cols[None, :]).astype(jnp.float32)[:, None, None, :]
        row_weight = geometry_part[:, :, 2, :, None] * kernel(
            row_cells[None, None, None, :] + 0.5 - geometry_part[:, :, 0, :, None]
        )
        start = geometry_part[:, :, 3, :, None]
        covered = (cells >= start) & (cells < start + FW)
        col_weight = jnp.where(covered, kernel(cells + 0.5 - geometry_part[:, :, 1, :, None]), 0.0)
        weights = (
            (row_weight[..., None] * col_weight[..., None, :])
            .reshape(senders, slot_count, block_len, slab_rows * UW)
            .astype(jnp.bfloat16)
        )
        windows = jnp.einsum(
            "stqc,stqk->sck", values, weights, preferred_element_type=jnp.float32
        ).reshape(senders, columns, slab_rows, UW)
        shifted = sender_base[:, None, None] + window_cols[None, :, None]
        placement = (shifted == grid_cols[None, None, :]).astype(jnp.float32)
        return running + jnp.einsum(
            "scij,sjg->cig", windows, placement, precision=lax.Precision.HIGHEST
        )

    slab_grid = lax.fori_loop(
        0, slab_count // senders, add_block, jnp.zeros((columns, slab_rows, grid_len), jnp.float32)
    )
    cosine_table, sine_table = inverse_table(grid_len)
    layered = slab_grid.reshape(coil_dev, part_count, kz_len * slab_rows, grid_len)
    real_part = layered[:, 0].reshape(-1, grid_len)
    imag_part = layered[:, 1].reshape(-1, grid_len)
    row_real = (product(real_part, cosine_table) - product(imag_part, sine_table)).reshape(
        coil_dev, kz_len, slab_rows * grid_len
    )
    row_imag = (product(real_part, sine_table) + product(imag_part, cosine_table)).reshape(
        coil_dev, kz_len, slab_rows * grid_len
    )
    depth_cosine, depth_sine = inverse_table(kz_len)
    image_real = depth_product(row_real, depth_cosine) - depth_product(row_imag, depth_sine)
    image_imag = depth_product(row_real, depth_sine) + depth_product(row_imag, depth_cosine)
    images = jnp.stack([image_real, image_imag], axis=1).reshape(
        coil_dev, part_count, kz_len, slab_rows, grid_len
    )
    power_sum = jnp.transpose(jnp.sum(images * images, axis=(0, 1)), (1, 0, 2))
    coil_images = jnp.transpose(images, (3, 0, 1, 2, 4))
    total_power = lax.psum_scatter(power_sum, "coil", scatter_dimension=1, tiled=True)
    combined = jnp.sqrt(total_power)
    return (coil_images, combined)


def solution(mesh):
    return jax.shard_map(
        on_device,
        mesh=mesh,
        in_specs=(
            P("spoke", "coil", None, None, None),
            P("spoke", None, None),
            P("spoke", None),
            P("spoke"),
            P(),
            P("spoke", None),
            P(),
        ),
        out_specs=(P("spoke", "coil", None, None, None), P("spoke", "coil", None)),
        check_vma=False,
    )
```

profile of v0, /device:TPU:0, one launch (start us, length us, event | category | flops | bytes accessed | tf_op | source)
XLA Modules:
  0.0 308.9 jit_solution(3971556312023553615)
XLA Ops:
  7.2 0.7 compare_and_fusion.2
  7.9 0.7 compare_select_fusion.3
  9.5 0.7 convert_element_type.69
  10.3 0.8 fusion.93
  11.2 0.9 select_reduce_fusion
  12.4 1.1 gather_fusion.3
  13.5 1.1 gather_fusion.5
  14.7 1.1 gather_fusion.4
  16.3 0.6 gather_fusion.2
  16.9 0.8 reshape.342
  17.7 7.3 %all-to-all-start.1 = ((f32[8,1,1280]{2,1,0:T(1,128)}), f32[8,1,1280]{2,1,0:T(1,128)S(1)}, u32[]{:S(2)}, u32[]{:S(2)}) async-start(f32[8,1,1280]{2,1,0:T(1,128)} %reshape.342), calls=%async_computation.1 | async-start | bytes 81920 | tf_op jit(solution)/shard_map/all_to_all | solution.py:80
  25.1 1.2 dynamic_slice.7
  26.3 1.0 copy.89
  27.4 1.7 gather_fusion
  29.1 0.3 copy.90
  29.3 0.2 select_select_fusion
  29.6 0.6 gather_fusion.1
  30.2 1.3 select_bitcast_fusion
  32.1 6.0 %all-to-all-start = ((bf16[8,8,40,256]{3,2,0,1:T(8,128)(2,1)}), bf16[8,8,40,256]{3,2,0,1:T(8,128)(2,1)S(1)}, u32[]{:S(2)}, u32[]{:S(2)}) async-start(bf16[8,8,40,256]{3,2,0,1:T(8,128)(2,1)} %select_bitcast_fusion), calls=%async_computation | async-start | bytes 2621440 | tf_op jit(solution)/shard_map/all_to_all | solution.py:77
  38.4 0.5 broadcast.474
  38.9 0.7 reduce.3
  40.1 0.7 multiply_multiply_fusion
  40.8 1.1 multiply_select_fusion
  41.9 13.5 %multiply_convert_fusion = bf16[8,8,40,32,48]{4,3,2,1,0:T(8,128)(2,1)} fusion(f32[8,8,40,48]{3,2,1,0:T(8,128)S(1)} %multiply_select_fusion, f32[8,8,40,32]{3,2,1,0:T(8,128)S(1)} %multiply_multiply_fusion), kind=kLoop, calls=%fused_computation.6 | loop fusion | flops 7864320 | bytes 8683520 | tf_op jit(solution)/shard_map/while/body/eval_jaxpr/convert_element_type | solution.py:104
  55.4 36.8 %convert_element_type.74 = bf16[8,8,40,1536]{3,2,1,0:T(8,128)(2,1)} reshape(bf16[8,8,40,32,48]{4,3,2,1,0:T(8,128)(2,1)} %multiply_convert_fusion) | data formatting | bytes 15728640 | tf_op jit(solution)/shard_map/while/body/eval_jaxpr/convert_element_type | solution.py:104
  92.2 11.6 %fusion.5 = f32[8,256,1536,1]{1,2,3,0:T(8,128)} fusion(bf16[8,8,40,1536]{3,2,1,0:T(8,128)(2,1)} %convert_element_type.74, bf16[8,8,40,256]{3,2,0,1:T(8,128)(2,1)S(1)} %all-to-all-done), kind=kOutput, calls=%fused_computation.17 | convolution fusion | flops 2013265920 | bytes 21757952 | tf_op jit(solution)/shard_map/while/body/eval_jaxpr/stqc,stqk->sck/dot_general | solution.py:106
  103.8 28.7 %copy.99 = f32[256,32,48,8]{1,0,3,2:T(8,128)} copy(f32[256,32,48,8]{0,2,1,3:T(8,128)} %bitcast.105) | data formatting | bytes 25165824 | tf_op jit(solution)/shard_map/while/body/eval_jaxpr/scij,sjg->cig/dot_general | solution.py:111
  132.5 40.6 %dot_general.38 = f32[2,2,2048,48,8]{2,1,0,4,3:T(2,128)} reshape(f32[256,32,48,8]{1,0,3,2:T(8,128)} %copy.99) | data formatting | bytes 25165824 | tf_op jit(solution)/shard_map/while/body/eval_jaxpr/scij,sjg->cig/dot_general | solution.py:111
  173.1 20.5 %fusion.2 = f32[2,2,2048,256]{3,2,1,0:T(8,128)S(1)} fusion(f32[2,2,2048,48,8]{2,1,0,4,3:T(2,128)} %dot_general.38, s32[8,48]{1,0:T(8,128)S(1)} %get-tuple-element.35), kind=kOutput, calls=%fused_computation.14 | convolution fusion | flops 9663774720 | bytes 20973056 | tf_op jit(solution)/shard_map/while/body/eval_jaxpr/scij,sjg->cig/dot_general | solution.py:111
  193.6 0.5 fusion.92
  194.2 7.4 %fusion.16 = f32[4096,256]{1,0:T(8,128)} fusion(f32[4096,256]{1,0:T(8,128)S(1)} %bitcast.108), kind=kOutput, calls=%fused_computation.39 | convolution fusion | flops 3222208512 | bytes 8388608 | tf_op jit(solution)/shard_map/dot_general | solution.py:28
  201.5 4.4 %fusion.15 = f32[4096,256]{1,0:T(8,128)S(1)} fusion(f32[4096,256]{1,0:T(8,128)S(1)} %bitcast.109), kind=kOutput, calls=%fused_computation.38 | convolution fusion | flops 3222208512 | bytes 8388608 | tf_op jit(solution)/shard_map/dot_general | solution.py:28
  206.0 6.9 %convolution_subtract_fusion.1 = f32[4096,256]{1,0:T(8,128)} fusion(f32[4096,256]{1,0:T(8,128)S(1)} %fusion.15, f32[4096,256]{1,0:T(8,128)S(1)} %bitcast.106), kind=kOutput, calls=%fused_computation.13 | convolution fusion | flops 3223257088 | bytes 12582912 | tf_op jit(solution)/shard_map/dot_general | solution.py:28
  212.9 5.1 %reshape.275 = f32[2,64,8192]{2,1,0:T(8,128)} reshape(f32[4096,256]{1,0:T(8,128)} %convolution_subtract_fusion.1) | data formatting | bytes 8388608 | tf_op jit(solution)/shard_map/reshape | solution.py:122
  218.0 8.1 %fusion.29 = f32[64,2,8192]{2,0,1:T(8,128)} fusion(f32[2,64,8192]{2,1,0:T(8,128)} %reshape.275), kind=kOutput, calls=%fused_computation.61 | convolution fusion | flops 805367808 | bytes 8388608 | tf_op jit(solution)/shard_map/akg,kz->azg/dot_general | solution.py:32
  226.1 5.4 %fusion.33 = f32[64,2,8192]{2,0,1:T(8,128)} fusion(f32[2,64,8192]{2,1,0:T(8,128)S(1)} %copy-done.3), kind=kOutput, calls=%fused_computation.65 | convolution fusion | flops 805367808 | bytes 8388608 | tf_op jit(solution)/shard_map/akg,kz->azg/dot_general | solution.py:32
  231.5 6.9 %convolution_add_fusion.1 = f32[4096,256]{1,0:T(8,128)} fusion(f32[4096,256]{1,0:T(8,128)S(1)} %copy-done.5, f32[4096,256]{1,0:T(8,128)S(1)} %bitcast.107), kind=kOutput, calls=%fused_computation.12 | convolution fusion | flops 3223257088 | bytes 12582912 | tf_op jit(solution)/shard_map/dot_general | solution.py:28
  238.4 5.1 %reshape.276 = f32[2,64,8192]{2,1,0:T(8,128)} reshape(f32[4096,256]{1,0:T(8,128)} %convolution_add_fusion.1) | data formatting | bytes 8388608 | tf_op jit(solution)/shard_map/reshape | solution.py:125
  243.6 7.4 %convolution_subtract_fusion = f32[64,2,8192]{2,0,1:T(8,128)S(1)} fusion(f32[64,2,8192]{2,0,1:T(8,128)} %fusion.33, f32[2,64,8192]{2,1,0:T(8,128)} %reshape.276), kind=kOutput, calls=%fused_computation.10 | convolution fusion | flops 806416384 | bytes 12582912 | tf_op jit(solution)/shard_map/akg,kz->azg/dot_general | solution.py:32
  251.0 3.9 %convolution_add_fusion = f32[64,2,8192]{2,0,1:T(8,128)S(1)} fusion(f32[64,2,8192]{2,0,1:T(8,128)S(1)} %copy-done.6, f32[2,64,8192]{2,1,0:T(8,128)S(1)} %copy-done), kind=kOutput, calls=%fused_computation.9 | convolution fusion | flops 806416384 | bytes 12582912 | tf_op jit(solution)/shard_map/akg,kz->azg/dot_general | solution.py:32
  255.0 1.3 copy.110
  256.3 1.3 copy.109
  257.6 2.7 copy_dynamic-update-slice_fusion.1
  260.3 2.7 copy_dynamic-update-slice_fusion
  263.0 2.9 multiply_reduce_fusion
  265.9 1.2 copy-done.4
  267.1 32.7 %reduce-scatter.2.cloned.1.call-done = f32[32,16,256]{2,1,0:T(8,128)} async-done(((f32[32,64,256]{2,1,0:T(8,128)}), f32[32,16,256]{2,1,0:T(8,128)}) %reduce-scatter.2.cloned.1.call-update) | async-done | bytes 524304 | tf_op jit(solution)/shard_map/reduce_scatter | solution.py:136
  299.8 2.0 sqrt.3
  (52 shorter events, 2.2 us)
Async XLA Ops:
  7.2 19.2 %copy-start.7 = (bf16[8,2,2,64,256]{4,3,2,1,0:T(8,128)(2,1)S(1)}, bf16[8,2,2,64,256]{4,3,2,1,0:T(8,128)(2,1)}, u32[]{:S(2)}) copy-start(bf16[8,2,2,64,256]{4,3,2,1,0:T(8,128)(2,1)} %param.9) | copy-start | bytes 3145732
  17.7 14.4 %all-to-all-start.1 = ((f32[8,1,1280]{2,1,0:T(1,128)}), f32[8,1,1280]{2,1,0:T(1,128)S(1)}, u32[]{:S(2)}, u32[]{:S(2)}) async-start(f32[8,1,1280]{2,1,0:T(1,128)} %reshape.342), calls=%async_computation.1 | async-start | bytes 81920 | tf_op jit(solution)/shard_map/all_to_all | solution.py:80
  32.1 60.1 %all-to-all-start = ((bf16[8,8,40,256]{3,2,0,1:T(8,128)(2,1)}), bf16[8,8,40,256]{3,2,0,1:T(8,128)(2,1)S(1)}, u32[]{:S(2)}, u32[]{:S(2)}) async-start(bf16[8,8,40,256]{3,2,0,1:T(8,128)(2,1)} %select_bitcast_fusion), calls=%async_computation | async-start | bytes 2621440 | tf_op jit(solution)/shard_map/all_to_all | solution.py:77
  38.2 261.7 %reduce-scatter.2.cloned.1.call-start = ((), (), s32[]{:S(2)}) async-start(), calls=%async_computation.3 | async-start | bytes 2621440 | tf_op jit(solution)/shard_map/reduce_scatter | solution.py:136
  194.2 11.8 %copy-start.1 = (f32[2,1,2048,256]{3,2,1,0:T(8,128)}, f32[2,1,2048,256]{3,2,1,0:T(8,128)S(1)}, u32[]{:S(2)}) copy-start(f32[2,1,2048,256]{3,2,1,0:T(8,128)S(1)} %get-tuple-element.19) | copy-start | bytes 12582916
  218.0 8.1 %copy-start.3 = (f32[2,64,8192]{2,1,0:T(8,128)S(1)}, f32[2,64,8192]{2,1,0:T(8,128)}, u32[]{:S(2)}) copy-start(f32[2,64,8192]{2,1,0:T(8,128)} %reshape.275) | copy-start | bytes 12582916
  226.1 5.4 %copy-start.2 = (f32[2,1,2048,256]{3,2,1,0:T(8,128)S(1)}, f32[2,1,2048,256]{3,2,1,0:T(8,128)}, u32[]{:S(2)}) copy-start(f32[2,1,2048,256]{3,2,1,0:T(8,128)} %copy-done.1) | copy-start | bytes 12582916
  226.1 5.4 %copy-start.5 = (f32[4096,256]{1,0:T(8,128)S(1)}, f32[4096,256]{1,0:T(8,128)}, u32[]{:S(2)}) copy-start(f32[4096,256]{1,0:T(8,128)} %fusion.16) | copy-start | bytes 12582916
  243.6 7.5 %copy-start = (f32[2,64,8192]{2,1,0:T(8,128)S(1)}, f32[2,64,8192]{2,1,0:T(8,128)}, u32[]{:S(2)}) copy-start(f32[2,64,8192]{2,1,0:T(8,128)} %reshape.276) | copy-start | bytes 12582916
  243.6 7.5 %copy-start.6 = (f32[64,2,8192]{2,0,1:T(8,128)S(1)}, f32[64,2,8192]{2,0,1:T(8,128)}, u32[]{:S(2)}) copy-start(f32[64,2,8192]{2,0,1:T(8,128)} %fusion.29) | copy-start | bytes 12582916
  263.0 4.0 %copy-start.4 = (f32[2,2,64,32,256]{4,2,1,0,3:T(8,128)}, f32[2,2,64,32,256]{4,2,1,0,3:T(8,128)S(1)}, u32[]{:S(2)}) copy-start(f32[2,2,64,32,256]{4,2,1,0,3:T(8,128)S(1)} %copy_dynamic-update-slice_fusion) | copy-start | bytes 25165828
Sparse Core Ops, SparseCore 0:
  267.2 32.5 reduce-scatter.1
where the time goes:
time: 315 us; the launch traced here: 309 us
  local copies, waits for them, and re-layouts  140 us (44%)
  matrix products  82.5 us (26%)
  waiting for transfers between devices  32.8 us (10%)
  other arithmetic  24.2 us (8%)
  between operations  16 us (5%)
  starting transfers between devices  13.5 us (4%)
    dot_general x2, local copies, waits for them, and re-layouts, add_block(): jnp.einsum('scij,sjg->cig', windows, placement, precision=lax.Precision.H...  69.3 us
    convert_element_type x1, local copies, waits for them, and re-layouts, add_block(): weights = (row_weight[..., None] * col_weight[..., None, :]).reshape(send...  36.8 us
    reduce_scatter x1, waiting for transfers between devices, on_device(): lax.psum_scatter(power_sum, 'coil', scatter_dimension=1, tiled=True)  32.7 us
    dot_general x4, matrix products, product(): jnp.dot(left, right, precision=lax.Precision.HIGHEST, preferred_element_t...  25.6 us
    dot_general x4, matrix products, depth_product(): jnp.einsum('akg,kz->azg', left, right, precision=lax.Precision.HIGHEST)  24.9 us
    dot_general x1, matrix products, add_block(): jnp.einsum('scij,sjg->cig', windows, placement, precision=lax.Precision.H...  20.5 us
    convert_element_type x1, other arithmetic, add_block(): weights = (row_weight[..., None] * col_weight[..., None, :]).reshape(send...  13.5 us
    dot_general x1, matrix products, add_block(): jnp.einsum('stqc,stqk->sck', values, weights, preferred_element_type=jnp....  11.6 us
  transfers between devices with their start and end apart: 3, of which 1 were waited for; matrix products, arithmetic and copies ran while one was open for 19% of the time, Pallas kernels for 0%

commit v1 on v0

v1 whole, which is shorter than its diff:
```python
import functools
import math

import jax
import jax.numpy as jnp
import numpy as np
from jax import lax
from jax.experimental import pallas as pl
from jax.experimental.pallas import tpu as pltpu
from jax.sharding import PartitionSpec as P

FW = 32
REACH = 2
ROWS_STEP = 4


def kernel(distance):
    inner = jnp.maximum(1.0 - distance * distance * 0.25, 0.0)
    return inner * inner


def inverse_matrix(length):
    counter = np.arange(length)
    phase = 2.0 * np.pi / length * (counter[:, None] * counter[None, :] % length)
    cosine = np.cos(phase) / math.sqrt(length)
    sine = np.sin(phase) / math.sqrt(length)
    return np.block([[cosine, sine], [-sine, cosine]])


def two_terms(table):
    high = table.astype(jnp.bfloat16)
    low = (table - high.astype(np.float64)).astype(jnp.bfloat16)
    return high, low


def slab_kernel(
    slab_ref, value_ref, geometry_ref, high_ref, low_ref, image_ref, power_ref, turned_ref, col_ref, row_ref, *, group
):
    step = pl.program_id(0)
    rows_step, coil_dev, _, kz_len, grid_len = image_ref.shape
    slab_rows, depth = row_ref.shape

    @pl.when(step == 0)
    def _():
        first_row = slab_ref[0] * slab_rows
        chunk = 2 * group
        for start in range(0, depth, chunk):
            part = slice(start, start + chunk)
            turned_ref[:, part] = value_ref[part, :].T
            geometry = geometry_ref[:, part]
            cells = lax.broadcasted_iota(jnp.int32, (grid_len, chunk), 0).astype(jnp.float32)
            begin = geometry[3:4]
            covered = (cells >= begin) & (cells < begin + FW)
            col_ref[:, part] = jnp.where(covered, kernel(cells + 0.5 - geometry[1:2]), 0.0)
            rows = (first_row + lax.broadcasted_iota(jnp.int32, (slab_rows, chunk), 0)).astype(jnp.float32)
            row_ref[:, part] = geometry[2:3] * kernel(rows + 0.5 - geometry[0:1])

    span = (2 + 2 * REACH) * group
    pieces = []
    for pair in range(rows_step // 2):
        row = step * rows_step + 2 * pair
        lanes = pl.ds(pl.multiple_of(row * group, 128), span)
        values = turned_ref[:, lanes]
        columns = col_ref[:, lanes]
        for half in range(2):
            weight = (row_ref[pl.ds(row + half, 1), lanes] * columns).astype(jnp.bfloat16)
            cells = lax.dot_general(
                values, weight, (((1,), (1,)), ((), ())), preferred_element_type=jnp.float32
            ).astype(jnp.bfloat16)
            for coil in range(coil_dev):
                base = coil * 2 * kz_len
                pieces.append(
                    jnp.concatenate([cells[base : base + kz_len], cells[base + kz_len : base + 2 * kz_len]], axis=1)
                )
    stacked = jnp.concatenate(pieces, axis=0)
    out = jnp.dot(stacked, high_ref[...], preferred_element_type=jnp.float32)
    out = out + jnp.dot(stacked, low_ref[...], preferred_element_type=jnp.float32)
    for row in range(rows_step):
        power = jnp.zeros((kz_len, grid_len), jnp.float32)
        for coil in range(coil_dev):
            base = (row * coil_dev + coil) * kz_len
            for part in range(2):
                image = out[base : base + kz_len, part * grid_len : (part + 1) * grid_len]
                image_ref[row, coil, part] = image
                power = power + image * image
        power_ref[row] = power.astype(power_ref.dtype)


def on_device(depth_tables, column_tables, kdata, coords, foot_offset, live_count, dcf_table, dcf_index, slab_owner):
    slot_count, coil_dev, part_count, kz_len, grid_len = kdata.shape
    slab_count = lax.axis_size("spoke")
    coil_count = lax.axis_size("coil")
    slab_rows = grid_len // slab_count
    block_len = slab_rows + 2 * REACH
    columns = coil_dev * part_count * kz_len
    group = slab_count * slot_count
    depth = block_len * group

    live_flag = (jnp.arange(slot_count, dtype=jnp.int32) < live_count[0]).astype(jnp.float32)
    table_hit = dcf_index[:, :, None] == jnp.arange(dcf_table.shape[0], dtype=jnp.int32)[None, None, :]
    density = jnp.sum(jnp.where(table_hit, dcf_table[None, None, :], 0.0), axis=2) * live_flag[:, None]

    picked = slab_owner[:, None] * slab_rows + jnp.arange(block_len, dtype=jnp.int32)[None, :]
    geometry = jnp.stack([coords[:, 0], coords[:, 1], density], axis=0)
    geometry = jnp.pad(geometry, ((0, 0), (0, 0), (REACH, REACH)))
    geometry = jnp.take(geometry, picked, axis=2)
    starts = jnp.broadcast_to(
        jnp.take(foot_offset, slab_owner, axis=1).astype(jnp.float32)[None, :, :, None],
        (1, slot_count, slab_count, block_len),
    )
    geometry = jnp.transpose(jnp.concatenate([geometry, starts], axis=0), (2, 0, 3, 1))
    got_geometry = lax.all_to_all(geometry, "spoke", split_axis=0, concat_axis=0, tiled=True)
    got_geometry = jnp.transpose(got_geometry, (1, 2, 0, 3)).reshape(4, depth)

    samples = kdata.reshape(slot_count, columns, grid_len)
    turned = sum(
        jnp.einsum("tcs,cd->std", samples, table, preferred_element_type=jnp.float32) for table in depth_tables
    ).astype(jnp.bfloat16)
    turned = jnp.pad(turned, ((REACH, REACH), (0, 0), (0, 0)))
    blocks = jnp.take(turned, picked, axis=0)
    got = lax.all_to_all(blocks, "spoke", split_axis=0, concat_axis=0, tiled=True)
    got = jnp.transpose(got, (1, 0, 2, 3)).reshape(depth, columns)

    owned_slab = slab_owner[lax.axis_index("spoke")].reshape(1)
    rows_step = min(ROWS_STEP, slab_rows)
    whole = lambda shape: pl.BlockSpec(shape, lambda step: (0,) * len(shape))
    images, power = pl.pallas_call(
        functools.partial(slab_kernel, group=group),
        grid=(slab_rows // rows_step,),
        in_specs=[
            pl.BlockSpec(memory_space=pltpu.SMEM),
            whole((depth, columns)),
            whole((4, depth)),
            whole((2 * grid_len, 2 * grid_len)),
            whole((2 * grid_len, 2 * grid_len)),
        ],
        out_specs=[
            pl.BlockSpec((rows_step, coil_dev, part_count, kz_len, grid_len), lambda step: (step, 0, 0, 0, 0)),
            pl.BlockSpec((rows_step, kz_len, grid_len), lambda step: (step, 0, 0)),
        ],
        out_shape=[
            jax.ShapeDtypeStruct((slab_rows, coil_dev, part_count, kz_len, grid_len), jnp.float32),
            jax.ShapeDtypeStruct((slab_rows, kz_len, grid_len), jnp.bfloat16),
        ],
        scratch_shapes=[
            pltpu.VMEM((columns, depth), jnp.bfloat16),
            pltpu.VMEM((grid_len, depth), jnp.float32),
            pltpu.VMEM((slab_rows, depth), jnp.float32),
        ],
        compiler_params=pltpu.CompilerParams(dimension_semantics=("arbitrary",)),
    )(owned_slab, got, got_geometry, *column_tables)

    power = lax.all_to_all(power, "coil", split_axis=1, concat_axis=0, tiled=True)
    power = power.reshape(coil_count, slab_rows, kz_len // coil_count, grid_len)
    combined = jnp.sqrt(jnp.sum(power.astype(jnp.float32), axis=0))
    return (images, combined)


def solution(mesh):
    def run(kdata, *rest):
        coil_dev = kdata.shape[1] // mesh.shape["coil"]
        depth_tables = two_terms(np.kron(np.eye(coil_dev), inverse_matrix(kdata.shape[3])))
        column_tables = two_terms(inverse_matrix(kdata.shape[4]))
        return jax.shard_map(
            functools.partial(on_device, depth_tables, column_tables),
            mesh=mesh,
            in_specs=(
                P("spoke", "coil", None, None, None),
                P("spoke", None, None),
                P("spoke", None),
                P("spoke"),
                P(),
                P("spoke", None),
                P(),
            ),
            out_specs=(P("spoke", "coil", None, None, None), P("spoke", "coil", None)),
            check_vma=False,
        )(kdata, *rest)

    return run
```

time: 315 us -> 91.7 us (0.29); the launches traced: 309 us -> 91.1 us
  local copies, waits for them, and re-layouts: 140 us -> 15.5 us
  matrix products: 82.5 us -> 1.13 us
  other arithmetic: 24.2 us -> 4.89 us
  blocking collectives: 0 us -> 17 us
  between operations: 16 us -> 1.47 us
  Pallas kernels: 0 us -> 12.9 us
  waiting for transfers between devices: 32.8 us -> 26.2 us
    dot_general x10 -> x2, matrix products: 82.5 us -> 1.13 us  [on_device(): jnp.einsum('tcs,cd->std', samples, table, preferred_element_type=jnp.floa...]
    dot_general x2 -> x0, local copies, waits for them, and re-layouts: 69.3 us -> none  [add_block(): jnp.einsum('scij,sjg->cig', windows, placement, precision=lax.Precision.H...]
    convert_element_type x2 -> x1, local copies, waits for them, and re-layouts: 36.8 us -> 0.07 us  [on_device(): jnp.take(foot_offset, slab_owner, axis=1).astype(jnp.float32)]
    reduce_scatter x1 -> x0, waiting for transfers between devices: 32.7 us -> none  [on_device(): lax.psum_scatter(power_sum, 'coil', scatter_dimension=1, tiled=True)]
    all_to_all x2, waiting for transfers between devices: 0.01 us -> 26.2 us  [the longest x1 24.8 us: on_device(): lax.all_to_all(blocks, 'spoke', split_axis=0, concat_axis=0, tiled=True)]
    all_to_all x0 -> x1, blocking collectives: none -> 17 us  [on_device(): lax.all_to_all(power, 'coil', split_axis=1, concat_axis=0, tiled=True)]
    convert_element_type x3 -> x1, other arithmetic: 14.2 us -> 0.07 us  [on_device(): jnp.take(foot_offset, slab_owner, axis=1).astype(jnp.float32)]
    pallas_call x0 -> x1, Pallas kernels: none -> 12.9 us  [on_device(): pl.pallas_call(functools.partial(slab_kernel, group=group), grid=(slab_ro...]
  transfers between devices with their start and end apart: 3 -> 2, of which waited for: 1 -> 2; matrix products, arithmetic and copies ran while one was open for 19% -> 9% of each run, Pallas kernels for 0% -> 0%
where the time goes in v1:
time: 91.7 us; the launch traced here: 91.1 us
  waiting for transfers between devices  26.2 us (29%)
  blocking collectives  17 us (19%)
  local copies, waits for them, and re-layouts  15.5 us (17%)
  Pallas kernels  12.9 us (14%)
  starting transfers between devices  12 us (13%)
  other arithmetic  4.89 us (5%)
  between operations  1.47 us (2%)
  matrix products  1.13 us (1%)
    all_to_all x1, waiting for transfers between devices, on_device(): lax.all_to_all(blocks, 'spoke', split_axis=0, concat_axis=0, tiled=True)  24.8 us
    all_to_all x1, blocking collectives, on_device(): lax.all_to_all(power, 'coil', split_axis=1, concat_axis=0, tiled=True)  17 us
    pallas_call x1, Pallas kernels, on_device(): pl.pallas_call(functools.partial(slab_kernel, group=group), grid=(slab_ro...  12.9 us
    all_to_all x1, starting transfers between devices, on_device(): lax.all_to_all(geometry, 'spoke', split_axis=0, concat_axis=0, tiled=True)  7.28 us
    all_to_all x1, starting transfers between devices, on_device(): lax.all_to_all(blocks, 'spoke', split_axis=0, concat_axis=0, tiled=True)  4.71 us
    unnamed x13, local copies, waits for them, and re-layouts  3.74 us
    gather x2, local copies, waits for them, and re-layouts, on_device(): geometry = jnp.take(geometry, picked, axis=2)  2.37 us
  transfers between devices with their start and end apart: 2, of which 2 were waited for; matrix products, arithmetic and copies ran while one was open for 9% of the time, Pallas kernels for 0%

profile of v1, /device:TPU:0, one launch (start us, length us, event | category | flops | bytes accessed | tf_op | source)
XLA Modules:
  0.0 91.1 jit_solution(8190964693616121467)
XLA Ops:
  0.6 0.0 copy-start
  0.6 0.8 compare_and_fusion
  1.4 0.7 compare_select_fusion.2
  2.1 0.1 fusion.3
  2.1 0.1 compare_select_fusion
  2.9 0.1 reshape.137
  3.0 0.8 copy.63
  3.7 0.6 gather_fusion.2
  4.3 0.1 convert_bitcast_fusion
  4.4 0.1 copy.64
  4.4 0.8 fusion.4
  5.2 0.9 %select_reduce_fusion = f32[8,256]{1,0:T(8,128)S(1)} fusion(f32[129]{0:T(256)} %param.15, s32[8,256]{1,0:T(8,128)} %param.16), kind=kLoop, calls=%fused_computation.7 | loop fusion | flops 790528 | bytes 16900 | tf_op jit(solution)/shard_map/reduce_sum | solution.py:101
  6.2 0.1 bitcast_multiply_fusion
  6.2 0.2 copy.61
  6.5 0.1 pad.9
  6.6 0.0 copy-start.2
  6.6 2.1 %gather_fusion.1 = f32[288,3,8]{2,1,0:T(4,128)S(1)} fusion(f32[3,8,260]{1,0,2:T(4,128)S(1)} %pad.9, s32[1024]{0:T(1024)S(1)} %pad_clamp_fusion.1), kind=kCustom, calls=%fused_computation.1 | custom fusion | bytes 56448 | tf_op jit(solution)/shard_map/jit(_take)/gather | solution.py:106
  8.7 0.2 copy.71
  9.0 0.1 broadcast_in_dim.65
  9.1 0.8 reshape.164
  9.9 7.3 %all-to-all-start.1 = ((f32[8,1,1152]{2,1,0:T(1,128)}), f32[8,1,1152]{2,1,0:T(1,128)S(1)}, u32[]{:S(2)}, u32[]{:S(2)}) async-start(f32[8,1,1152]{2,1,0:T(1,128)} %reshape.164), calls=%async_computation.1 | async-start | bytes 73728 | tf_op jit(solution)/shard_map/all_to_all | solution.py:112
  17.2 0.0 copy-done
  17.2 0.0 copy-done.2
  17.2 0.0 copy-start.1
  17.2 0.6 fusion.5
  17.8 0.3 copy-done.1
  18.1 0.6 fusion
  18.7 0.6 copy.74
  19.3 0.1 pad.8.clone
  19.4 1.8 %gather_fusion = bf16[288,8,256]{2,1,0:T(8,128)(2,1)S(1)} fusion(bf16[260,8,256]{2,1,0:T(8,128)(2,1)S(1)} %pad.8.clone, s32[1024]{0:T(1024)S(1)} %pad_clamp_fusion.1), kind=kCustom, calls=%fused_computation | custom fusion | bytes 2360448 | tf_op jit(solution)/shard_map/jit(_take)/gather | solution.py:120
  21.2 1.3 %broadcast_select_fusion = bf16[8,36,8,256]{3,2,1,0:T(8,128)(2,1)} fusion(bf16[8,36,8,256]{3,2,1,0:T(8,128)(2,1)S(1)} %bitcast.44, pred[8,36]{1,0:T(8,128)(4,1)S(1)} %fusion.3), kind=kLoop, calls=%fused_computation.6 | loop fusion | flops 589824 | bytes 2359584 | tf_op jit(solution)/shard_map/jit(_take)/select_n | solution.py:120
  22.5 1.4 %all-to-all-done.1 = f32[8,1,1152]{2,1,0:T(1,128)S(1)} async-done(((f32[8,1,1152]{2,1,0:T(1,128)}), f32[8,1,1152]{2,1,0:T(1,128)S(1)}, u32[]{:S(2)}, u32[]{:S(2)}) %all-to-all-start.1) | async-done | bytes 36896 | tf_op jit(solution)/shard_map/all_to_all | solution.py:112
  23.9 4.7 %all-to-all-start = ((bf16[8,36,8,256]{3,2,1,0:T(8,128)(2,1)}), bf16[8,36,8,256]{3,2,1,0:T(8,128)(2,1)S(1)}, u32[]{:S(2)}, u32[]{:S(2)}) async-start(bf16[8,36,8,256]{3,2,1,0:T(8,128)(2,1)} %broadcast_select_fusion), calls=%async_computation | async-start | bytes 2359296 | tf_op jit(solution)/shard_map/all_to_all | solution.py:121
  28.6 0.0 copy-done.3
  28.6 0.7 dynamic_slice.3.slab_ref
  29.3 0.5 broadcast.134
  29.8 0.7 reduce.1
  30.5 0.2 reshape.165
  30.7 0.3 copy.66
  31.0 0.9 %reshape.133.geometry_ref = f32[4,2304]{1,0:T(4,128)} reshape(f32[4,36,8,8]{3,2,1,0:T(8,128)S(1)} %copy.66) | data formatting | bytes 73728 | tf_op jit(solution)/shard_map/reshape | solution.py:113
  32.0 24.8 %all-to-all-done = bf16[8,36,8,256]{3,2,1,0:T(8,128)(2,1)S(1)} async-done(((bf16[8,36,8,256]{3,2,1,0:T(8,128)(2,1)}), bf16[8,36,8,256]{3,2,1,0:T(8,128)(2,1)S(1)}, u32[]{:S(2)}, u32[]{:S(2)}) %all-to-all-start) | async-done | bytes 1179680 | tf_op jit(solution)/shard_map/all_to_all | solution.py:121
  56.8 1.2 %copy.58 = bf16[36,8,8,256]{3,2,1,0:T(8,128)(2,1)} copy(bf16[36,8,8,256]{3,2,0,1:T(8,128)(2,1)S(1)} %bitcast.43) | data formatting | bytes 2359296 | tf_op jit(solution)/shard_map/transpose | solution.py:122
  58.0 12.9 %shard_map.122 = (f32[32,2,2,64,256]{4,3,2,1,0:T(8,128)}, bf16[32,64,256]{2,1,0:T(8,128)(2,1)}) custom-call(s32[1]{0:T(128)} %dynamic_slice.3.slab_ref, bf16[2304,256]{1,0:T(8,128)(2,1)} %bitcast.42, f32[4,2304]{1,0:T(4,128)} %reshape.133.geometry_ref, bf16[512,512]{1,0:T(8,128)(2,1)} %constant.67.clone.high_ref, bf16[512,512]{1,0:T(8,128)(2,1)} %constant.68.clone.low_ref), custom_call_target="tpu_custom_call" | custom-call | tf_op jit(solution)/shard_map/pallas_call | solution.py:127
  70.9 1.8 %copy.67 = bf16[32,64,256]{2,0,1:T(8,128)(2,1)S(1)} copy(bf16[32,64,256]{2,1,0:T(8,128)(2,1)} %get-tuple-element.5) | data formatting | bytes 2097152 | tf_op jit(solution)/shard_map/pallas_call | solution.py:127
  72.7 17.0 %all_to_all.19 = bf16[32,64,256]{2,0,1:T(8,128)(2,1)S(1)} all-to-all(bf16[32,64,256]{2,0,1:T(8,128)(2,1)S(1)} %copy.67), channel_id=1, replica_groups=mesh['coil'=4,'spoke'=8] {'coil'}, dimensions={1} | all-to-all | bytes 2097152 | tf_op jit(solution)/shard_map/all_to_all | solution.py:153
  89.7 0.2 convert_reduce_fusion
  89.9 0.1 sqrt.3
  90.0 1.1 %copy.68 = f32[32,16,256]{2,1,0:T(8,128)} copy(f32[32,16,256]{2,0,1:T(8,128)S(1)} %sqrt.3) | data formatting | bytes 1048576
  (10 shorter events, 0.1 us)
Async XLA Ops:
  0.6 16.6 %copy-start = (bf16[8,2,2,64,256]{4,3,2,1,0:T(8,128)(2,1)S(1)}, bf16[8,2,2,64,256]{4,3,2,1,0:T(8,128)(2,1)}, u32[]{:S(2)}) copy-start(bf16[8,2,2,64,256]{4,3,2,1,0:T(8,128)(2,1)} %param.11) | copy-start | bytes 3145732
  6.6 10.6 %copy-start.2 = (bf16[256,256,1]{1,0,2:T(8,128)(2,1)S(1)}, bf16[256,256,1]{1,0,2:T(8,128)(2,1)}, u32[]{:S(2)}) copy-start(bf16[256,256,1]{1,0,2:T(8,128)(2,1)} %constant.75) | copy-start | bytes 393220
  9.9 14.0 %all-to-all-start.1 = ((f32[8,1,1152]{2,1,0:T(1,128)}), f32[8,1,1152]{2,1,0:T(1,128)S(1)}, u32[]{:S(2)}, u32[]{:S(2)}) async-start(f32[8,1,1152]{2,1,0:T(1,128)} %reshape.164), calls=%async_computation.1 | async-start | bytes 73728 | tf_op jit(solution)/shard_map/all_to_all | solution.py:112
  17.2 0.9 copy-start.1
  22.5 6.1 %copy-start.3 = (s32[8]{0:T(128)S(1)}, s32[8]{0:T(128)}, u32[]{:S(2)}) copy-start(s32[8]{0:T(128)} %param.17) | copy-start | bytes 100
  23.9 32.9 %all-to-all-start = ((bf16[8,36,8,256]{3,2,1,0:T(8,128)(2,1)}), bf16[8,36,8,256]{3,2,1,0:T(8,128)(2,1)S(1)}, u32[]{:S(2)}, u32[]{:S(2)}) async-start(bf16[8,36,8,256]{3,2,1,0:T(8,128)(2,1)} %broadcast_select_fusion), calls=%async_computation | async-start | bytes 2359296 | tf_op jit(solution)/shard_map/all_to_all | solution.py:121

commit v2 on v1

v2 whole, which is shorter than its diff:
```python
import functools
import math

import jax
import jax.numpy as jnp
import numpy as np
from jax import lax
from jax.experimental import pallas as pl
from jax.experimental.pallas import tpu as pltpu
from jax.sharding import PartitionSpec as P

FW = 32
REACH = 2
ROWS_STEP = 4


def kernel(distance):
    inner = jnp.maximum(1.0 - distance * distance * 0.25, 0.0)
    return inner * inner


def inverse_matrix(length):
    counter = np.arange(length)
    phase = 2.0 * np.pi / length * (counter[:, None] * counter[None, :] % length)
    cosine = np.cos(phase) / math.sqrt(length)
    sine = np.sin(phase) / math.sqrt(length)
    return np.block([[cosine, sine], [-sine, cosine]])


def two_terms(table):
    high = table.astype(jnp.bfloat16)
    low = (table - high.astype(np.float64)).astype(jnp.bfloat16)
    return high, low


def slab_kernel(place_ref, geometry_ref, high_ref, low_ref, *refs, group, value_count, alias_count):
    value_refs = refs[:value_count]
    image_ref, keep_ref, send_ref, turned_ref, col_ref, row_ref = refs[value_count + alias_count :]
    step = pl.program_id(0)
    rows_step, coil_dev, _, kz_len, grid_len = image_ref.shape
    chunk_rows, depth = row_ref.shape
    kz_part = keep_ref.shape[2]

    @pl.when(step == 0)
    def _():
        first_row = place_ref[0]
        chunk = 2 * group
        samples = [(ref, index) for ref in value_refs for index in range(ref.shape[1])]
        for start in range(0, depth, chunk):
            part = slice(start, start + chunk)
            taken = samples[start // group : start // group + 2]
            taken = [ref[:, index].reshape(group, ref.shape[3]) for ref, index in taken]
            turned_ref[:, part] = jnp.concatenate(taken, axis=0).T
            geometry = geometry_ref[:, part]
            cells = lax.broadcasted_iota(jnp.int32, (grid_len, chunk), 0).astype(jnp.float32)
            begin = geometry[3:4]
            covered = (cells >= begin) & (cells < begin + FW)
            col_ref[:, part] = jnp.where(covered, kernel(cells + 0.5 - geometry[1:2]), 0.0)
            rows = (first_row + lax.broadcasted_iota(jnp.int32, (chunk_rows, chunk), 0)).astype(jnp.float32)
            row_ref[:, part] = geometry[2:3] * kernel(rows + 0.5 - geometry[0:1])

    span = (2 + 2 * REACH) * group
    pieces = []
    for pair in range(rows_step // 2):
        row = step * rows_step + 2 * pair
        lanes = pl.ds(pl.multiple_of(row * group, 128), span)
        values = turned_ref[:, lanes]
        columns = col_ref[:, lanes]
        for half in range(2):
            weight = (row_ref[pl.ds(row + half, 1), lanes] * columns).astype(jnp.bfloat16)
            cells = lax.dot_general(
                values, weight, (((1,), (1,)), ((), ())), preferred_element_type=jnp.float32
            ).astype(jnp.bfloat16)
            for coil in range(coil_dev):
                base = coil * 2 * kz_len
                pieces.append(
                    jnp.concatenate([cells[base : base + kz_len], cells[base + kz_len : base + 2 * kz_len]], axis=1)
                )
    stacked = jnp.concatenate(pieces, axis=0)
    out = jnp.dot(stacked, high_ref[...], preferred_element_type=jnp.float32)
    out = out + jnp.dot(stacked, low_ref[...], preferred_element_type=jnp.float32)
    first_core = place_ref[1] == 0
    for row in range(rows_step):
        power = jnp.zeros((kz_len, grid_len), jnp.float32)
        for coil in range(coil_dev):
            base = (row * coil_dev + coil) * kz_len
            for part in range(2):
                image = out[base : base + kz_len, part * grid_len : (part + 1) * grid_len]
                image_ref[row, coil, part] = image
                power = power + image * image
        for chip in range(keep_ref.shape[0]):
            one = power[2 * chip * kz_part : (2 * chip + 1) * kz_part]
            two = power[(2 * chip + 1) * kz_part : (2 * chip + 2) * kz_part]
            keep_ref[chip, row] = jnp.where(first_core, one, two)
            send_ref[chip, row] = jnp.where(first_core, two, one).astype(send_ref.dtype)


def image_chunk(done, place, values, geometry, column_tables, shape, first, rows, chips):
    slab_rows, coil_dev, part_count, kz_len, grid_len = shape
    depth = geometry.shape[1]
    columns = coil_dev * part_count * kz_len
    slab_count, _, slot_count, _ = values[0][0].shape
    group = slab_count * slot_count
    kz_part = kz_len // (2 * chips)
    offset = first // ROWS_STEP
    whole = lambda size: pl.BlockSpec(size, lambda step: (0,) * len(size))
    samples = lambda count, at: pl.BlockSpec((slab_count, count, slot_count, columns), lambda step: (0, at, 0, 0))
    halves = pl.BlockSpec((chips, ROWS_STEP, kz_part, grid_len), lambda step: (0, step + offset, 0, 0))
    macs = rows * columns * grid_len * (6 * group + 4 * grid_len)
    return pl.pallas_call(
        functools.partial(slab_kernel, group=group, value_count=len(values), alias_count=len(done)),
        grid=(rows // ROWS_STEP,),
        in_specs=[
            pl.BlockSpec(memory_space=pltpu.SMEM),
            whole((4, depth)),
            whole((2 * grid_len, 2 * grid_len)),
            whole((2 * grid_len, 2 * grid_len)),
        ]
        + [samples(count, at) for _, count, at in values]
        + [pl.BlockSpec(memory_space=pl.ANY)] * len(done),
        out_specs=[
            pl.BlockSpec((ROWS_STEP, coil_dev, part_count, kz_len, grid_len), lambda step: (step + offset, 0, 0, 0, 0)),
            halves,
            halves,
        ],
        out_shape=[
            jax.ShapeDtypeStruct(shape, jnp.float32),
            jax.ShapeDtypeStruct((chips, slab_rows, kz_part, grid_len), jnp.float32),
            jax.ShapeDtypeStruct((chips, slab_rows, kz_part, grid_len), jnp.bfloat16),
        ],
        scratch_shapes=[
            pltpu.VMEM((columns, depth), jnp.bfloat16),
            pltpu.VMEM((grid_len, depth), jnp.float32),
            pltpu.VMEM((rows, depth), jnp.float32),
        ],
        input_output_aliases={4 + len(values) + i: i for i in range(len(done))},
        cost_estimate=pl.CostEstimate(
            flops=2 * macs, bytes_accessed=rows * columns * grid_len * 4, transcendentals=0
        ),
        compiler_params=pltpu.CompilerParams(dimension_semantics=("arbitrary",)),
    )(place, geometry, *column_tables, *[array for array, _, _ in values], *done)


def coil_sum(keep, send, chips):
    count = 2 * chips
    me = lax.axis_index("coil")
    chip = me // 2
    got = lax.ppermute(send, "coil", [(i, i ^ 1) for i in range(count)])
    both = keep + got.astype(jnp.float32)
    total = lax.dynamic_index_in_dim(both, chip, 0, keepdims=False)
    for turn in range(1, chips):
        block = lax.dynamic_index_in_dim(both, (chip + turn) % chips, 0, keepdims=False).astype(jnp.bfloat16)
        got = lax.ppermute(block, "coil", [(i, (i + 2 * turn) % count) for i in range(count)])
        total = total + got.astype(jnp.float32)
    return jnp.sqrt(total)


def on_device(depth_tables, column_tables, kdata, coords, foot_offset, live_count, dcf_table, dcf_index, slab_owner):
    slot_count, coil_dev, part_count, kz_len, grid_len = kdata.shape
    slab_count = lax.axis_size("spoke")
    chips = lax.axis_size("coil") // 2
    slab_rows = grid_len // slab_count
    block_len = slab_rows + 2 * REACH
    columns = coil_dev * part_count * kz_len
    group = slab_count * slot_count
    second = max(ROWS_STEP, slab_rows * 3 // 8 // ROWS_STEP * ROWS_STEP)
    first = slab_rows - second
    edge = first + 2 * REACH

    samples = kdata.reshape(slot_count, columns, grid_len)
    turned = sum(
        jnp.einsum("tcs,cd->std", samples, table, preferred_element_type=jnp.float32) for table in depth_tables
    ).astype(jnp.bfloat16)
    turned = jnp.pad(turned, ((REACH, REACH), (0, 0), (0, 0)))
    picked = slab_owner[:, None] * slab_rows + jnp.arange(block_len, dtype=jnp.int32)[None, :]
    sent = [jnp.take(turned, part, axis=0, mode="clip") for part in (picked[:, :edge], picked[:, edge:])]
    got_first = lax.all_to_all(sent[0], "spoke", split_axis=0, concat_axis=0, tiled=True)
    got_second = lax.all_to_all(sent[1], "spoke", split_axis=0, concat_axis=0, tiled=True)

    coords, dcf_index, _ = lax.optimization_barrier((coords, dcf_index, sent[0]))
    live_flag = (jnp.arange(slot_count, dtype=jnp.int32) < live_count[0]).astype(jnp.float32)
    table_hit = dcf_index[:, :, None] == jnp.arange(dcf_table.shape[0], dtype=jnp.int32)[None, None, :]
    density = jnp.sum(jnp.where(table_hit, dcf_table[None, None, :], 0.0), axis=2) * live_flag[:, None]
    starts = jnp.pad(foot_offset.astype(jnp.float32), ((0, 0), (0, grid_len - slab_count)))
    geometry = jnp.stack([coords[:, 0], coords[:, 1], density, starts], axis=0)
    geometry = lax.all_gather(geometry, "spoke", axis=1, tiled=True)

    owned_slab = slab_owner[lax.axis_index("spoke")]
    first_row = owned_slab * slab_rows
    starts = lax.dynamic_slice(geometry, (3, 0, owned_slab), (1, group, 1))
    near = lax.dynamic_slice_in_dim(
        jnp.pad(geometry[:3], ((0, 0), (0, 0), (REACH, REACH))), first_row, block_len, axis=2
    )
    geometry = jnp.concatenate([near, jnp.broadcast_to(starts, (1, group, block_len))], axis=0)
    geometry = jnp.transpose(geometry, (0, 2, 1)).reshape(4, block_len * group)

    core = lax.axis_index("coil") % 2
    place = jnp.stack([first_row, core]).astype(jnp.int32)
    shape = (slab_rows, coil_dev, part_count, kz_len, grid_len)
    done = image_chunk(
        (), place, [(got_first, edge, 0)], geometry[:, : edge * group], column_tables, shape, 0, first, chips
    )
    place = jnp.stack([first_row + first, core]).astype(jnp.int32)
    values = [(got_first, 2 * REACH, first // (2 * REACH)), (got_second, second, 0)]
    images, keep, send = image_chunk(
        done, place, values, geometry[:, first * group :], column_tables, shape, first, second, chips
    )
    return (images, coil_sum(keep, send, chips))


def solution(mesh):
    def run(kdata, *rest):
        coil_dev = kdata.shape[1] // mesh.shape["coil"]
        depth_tables = two_terms(np.kron(np.eye(coil_dev), inverse_matrix(kdata.shape[3])))
        column_tables = two_terms(inverse_matrix(kdata.shape[4]))
        return jax.shard_map(
            functools.partial(on_device, depth_tables, column_tables),
            mesh=mesh,
            in_specs=(
                P("spoke", "coil", None, None, None),
                P("spoke", None, None),
                P("spoke", None),
                P("spoke"),
                P(),
                P("spoke", None),
                P(),
            ),
            out_specs=(P("spoke", "coil", None, None, None), P("spoke", "coil", None)),
            check_vma=False,
        )(kdata, *rest)

    return run
```

time: 91.7 us -> 93.5 us (1.020)
  blocking collectives: 17 us -> 38.2 us
  waiting for transfers between devices: 26.2 us -> 8.94 us
  local copies, waits for them, and re-layouts: 15.5 us -> 7.54 us
  between operations: 1.47 us -> 4.08 us
  Pallas kernels: 12.9 us -> 14.9 us
    all_gather x0 -> x1, blocking collectives: none -> 38.2 us  [on_device(): geometry = lax.all_gather(geometry, 'spoke', axis=1, tiled=True)]
    all_to_all x2, waiting for transfers between devices: 26.2 us -> 0.01 us  [the longest x1 0.01 us: on_device(): lax.all_to_all(sent[0], 'spoke', split_axis=0, concat_axis=0, tiled=True)]
    all_to_all x1 -> x0, blocking collectives: 17 us -> none  [on_device(): lax.all_to_all(power, 'coil', split_axis=1, concat_axis=0, tiled=True)]
    ppermute x0 -> x2, waiting for transfers between devices: none -> 8.93 us  [the longest x1 6.82 us: coil_sum(): lax.ppermute(block, 'coil', [(i, (i + 2 * turn) % count) for i in range(c...]
    select_n x4 -> x0, other arithmetic: 2.05 us -> none  [the longest x2 1.37 us: on_device(): blocks = jnp.take(turned, picked, axis=0)]
    unnamed x13 -> x19, local copies, waits for them, and re-layouts: 3.74 us -> 1.73 us
    pallas_call x1 -> x2, Pallas kernels: 12.9 us -> 14.9 us  [image_chunk(): pl.pallas_call(functools.partial(slab_kernel, group=group, value_count=le...]
    pallas_call x1 -> x0, local copies, waits for them, and re-layouts: 1.81 us -> none  [on_device(): pl.pallas_call(functools.partial(slab_kernel, group=group), grid=(slab_ro...]
  transfers between devices with their start and end apart: 2 -> 4, of which waited for: 2 -> 2; matrix products, arithmetic and copies ran while one was open for 9% -> 6% of each run, Pallas kernels for 0% -> 9%
where the time goes in v2:
time: 93.5 us; the launch traced here: 93 us
  blocking collectives  38.2 us (41%)
  Pallas kernels  14.9 us (16%)
  starting transfers between devices  12.5 us (13%)
  waiting for transfers between devices  8.94 us (10%)
  local copies, waits for them, and re-layouts  7.54 us (8%)
  other arithmetic  4.8 us (5%)
  between operations  4.08 us (4%)
  matrix products  2.06 us (2%)
    all_gather x1, blocking collectives, on_device(): geometry = lax.all_gather(geometry, 'spoke', axis=1, tiled=True)  38.2 us
    pallas_call x2, Pallas kernels, image_chunk(): pl.pallas_call(functools.partial(slab_kernel, group=group, value_count=le...  14.9 us
    all_to_all x1, starting transfers between devices, on_device(): lax.all_to_all(sent[0], 'spoke', split_axis=0, concat_axis=0, tiled=True)  7.42 us
    ppermute x1, waiting for transfers between devices, coil_sum(): lax.ppermute(block, 'coil', [(i, (i + 2 * turn) % count) for i in range(c...  6.82 us
    all_to_all x1, starting transfers between devices, on_device(): lax.all_to_all(sent[1], 'spoke', split_axis=0, concat_axis=0, tiled=True)  3.46 us
    gather x2, local copies, waits for them, and re-layouts, on_device(): jnp.take(turned, part, axis=0, mode='clip')  3.09 us
    ppermute x1, waiting for transfers between devices, coil_sum(): got = lax.ppermute(send, 'coil', [(i, i ^ 1) for i in range(count)])  2.11 us
    dot_general x2, matrix products, on_device(): jnp.einsum('tcs,cd->std', samples, table, preferred_element_type=jnp.floa...  2.06 us
  transfers between devices with their start and end apart: 4, of which 2 were waited for; matrix products, arithmetic and copies ran while one was open for 6% of the time, Pallas kernels for 9%

profile of v2, /device:TPU:0, one launch (start us, length us, event | category | flops | bytes accessed | tf_op | source)
XLA Modules:
  0.0 93.0 jit_solution(5913406527039633288)
XLA Ops:
  0.6 0.0 copy-start
  0.6 0.7 broadcast_multiply_fusion
  1.4 0.1 iota_add_fusion
  1.5 0.1 reshape.52
  1.6 0.3 copy-done
  1.9 1.5 %fusion.3 = f32[256,8,256]{0,2,1:T(8,128)S(1)} fusion(bf16[256,256,1]{1,0,2:T(8,128)(2,1)} %constant.82, bf16[8,256,256]{2,1,0:T(8,128)(2,1)S(1)} %bitcast.34), kind=kOutput, calls=%fused_computation.26 | convolution fusion | flops 268435456 | bytes 3276800 | tf_op jit(solution)/shard_map/tcs,cd->std/dot_general | solution.py:172
  3.4 0.0 copy-done.3
  3.4 0.6 fusion
  4.0 0.6 copy.39
  4.6 0.1 pad.12.clone
  4.6 1.7 %gather_fusion = bf16[192,8,256]{2,1,0:T(8,128)(2,1)} fusion(bf16[260,8,256]{2,1,0:T(8,128)(2,1)S(1)} %pad.12.clone, s32[1024]{0:T(1024)S(1)} %pad_clamp_fusion.1), kind=kCustom, calls=%fused_computation | custom fusion | bytes 1573632 | tf_op jit(solution)/shard_map/jit(_take)/gather | solution.py:176
  6.3 0.0 copy-start.7
  6.3 7.4 %all-to-all-start = ((bf16[8,24,8,256]{3,2,1,0:T(8,128)(2,1)}), bf16[8,24,8,256]{3,2,1,0:T(8,128)(2,1)S(1)}, u32[]{:S(2)}, u32[]{:S(2)}) async-start(bf16[8,24,8,256]{3,2,1,0:T(8,128)(2,1)} %bitcast.36), calls=%async_computation | async-start | bytes 1572864 | tf_op jit(solution)/shard_map/all_to_all | solution.py:177
  13.8 0.1 slice.26
  14.5 0.0 copy-done.8
  14.5 0.6 dynamic_slice.16
  15.7 0.1 reshape.60
  15.8 0.0 copy-done.6
  15.8 1.4 %gather_fusion.1 = bf16[96,8,256]{2,1,0:T(8,128)(2,1)} fusion(bf16[260,8,256]{2,1,0:T(8,128)(2,1)S(1)} %pad.12.clone, s32[1024]{0:T(1024)S(1)} %pad_clamp_fusion), kind=kCustom, calls=%fused_computation.1 | custom fusion | bytes 786816 | tf_op jit(solution)/shard_map/jit(_take)/gather | solution.py:176
  17.2 0.0 copy-done.4
  17.3 0.0 copy-done.5
  17.3 0.0 copy-done.7
  17.3 0.2 select_reduce_fusion
  17.5 0.1 bitcast_multiply_fusion
  17.6 38.2 %all_gather.3 = f32[4,64,256]{2,1,0:T(8,128)S(1)} all-gather(f32[4,8,256]{2,1,0:T(8,128)S(1)} %pad_maximum_fusion), channel_id=1, replica_groups=mesh['coil'=4,'spoke'=8] {'spoke'}, dimensions={1}, use_global_device_ids=true | all-gather | bytes 294912 | tf_op jit(solution)/shard_map/all_gather | solution.py:186
  55.8 0.0 all-to-all-done.refs_0_
  55.8 0.0 copy-start.1
  55.8 3.5 %all-to-all-start.1 = ((bf16[8,12,8,256]{3,2,1,0:T(8,128)(2,1)}), bf16[8,12,8,256]{3,2,1,0:T(8,128)(2,1)S(1)}, u32[]{:S(2)}, u32[]{:S(2)}) async-start(bf16[8,12,8,256]{3,2,1,0:T(8,128)(2,1)} %bitcast.14), calls=%async_computation.1 | async-start | bytes 786432 | tf_op jit(solution)/shard_map/all_to_all | solution.py:178
  59.3 0.1 pad_dynamic-slice_fusion
  61.4 0.2 dynamic-slice_reduce_fusion
  61.5 0.1 broadcast_in_dim.37
  61.6 0.1 copy.35
  61.7 0.1 reshape.49
  61.8 0.6 slice.35.geometry_ref
  62.5 0.6 slice.36.geometry_ref
  63.1 0.6 pad_add_fusion.place_ref
  63.7 0.7 pad_add_fusion.1.place_ref
  64.4 0.0 copy-done.1
  64.4 8.7 %shard_map.122 = (f32[32,2,2,64,256]{4,3,2,1,0:T(8,128)}, f32[2,32,16,256]{3,2,1,0:T(8,128)}, bf16[2,32,16,256]{3,2,1,0:T(8,128)(2,1)}) custom-call(s32[2]{0:T(128)} %pad_add_fusion.1.place_ref, f32[4,1536]{1,0:T(4,128)} %slice.36.geometry_ref, bf16[512,512]{1,0:T(8,128)(2,1)} %constant.72.clone.high_ref, bf16[512,512]{1,0:T(8,128)(2,1)} %constant.73.clone.low_ref, ...), custom_call_target="tpu_custom_call" | custom-call | flops 3690987520 | bytes 5242880 | tf_op jit(solution)/shard_map/pallas_call | solution.py:110
  73.1 0.0 all-to-all-done.1.refs_1_
  73.1 0.8 copy-done.2
  73.9 6.2 %shard_map.123 = (f32[32,2,2,64,256]{4,3,2,1,0:T(8,128)}, f32[2,32,16,256]{3,2,1,0:T(8,128)}, bf16[2,32,16,256]{3,2,1,0:T(8,128)(2,1)}) custom-call(s32[2]{0:T(128)} %pad_add_fusion.place_ref, f32[4,1024]{1,0:T(4,128)} %slice.35.geometry_ref, bf16[512,512]{1,0:T(8,128)(2,1)} %constant.72.clone.high_ref, ...), custom_call_target="tpu_custom_call", output_to_operand_aliasing={{0}: (6, {}), {1}: (7, {}), {2}: (8, {})} | custom-call | flops 2214592512 | bytes 3145728 | tf_op jit(solution)/shard_map/pallas_call | solution.py:110
  80.0 0.0 collective-permute-start
  80.0 2.1 %collective-permute-done = bf16[2,32,16,256]{3,2,1,0:T(8,128)(2,1)S(1)} collective-permute-done((bf16[2,32,16,256]{3,2,1,0:T(8,128)(2,1)}, bf16[2,32,16,256]{3,2,1,0:T(8,128)(2,1)S(1)}, u32[]{:S(2)}, u32[]{:S(2)}) %collective-permute-start) | collective-permute-done | bytes 524320 | tf_op jit(solution)/shard_map/ppermute | solution.py:148
  82.2 1.4 %convert_add_fusion = f32[2,32,16,256]{3,2,1,0:T(8,128)S(1)} fusion(f32[2,32,16,256]{3,2,1,0:T(8,128)} %get-tuple-element.16, bf16[2,32,16,256]{3,2,1,0:T(8,128)(2,1)S(1)} %collective-permute-done), kind=kLoop, calls=%fused_computation.6 | loop fusion | flops 524288 | bytes 2621440 | tf_op jit(solution)/shard_map/add | solution.py:149
  83.6 1.6 %collective-permute-start.1 = (bf16[32,16,256]{2,1,0:T(8,128)(2,1)S(1)}, bf16[32,16,256]{2,1,0:T(8,128)(2,1)S(1)}, u32[]{:S(2)}, u32[]{:S(2)}) collective-permute-start(bf16[32,16,256]{2,1,0:T(8,128)(2,1)S(1)} %fusion.2), channel_id=1, source_target_pairs={{0,16},{8,24},{16,0},{24,8},{1,17},{9,25},{17,1},{25,9},{2,18},{10... | collective-permute-start | bytes 786440 | tf_op jit(solution)/shard_map/ppermute | solution.py:153
  85.2 6.8 %collective-permute-done.1 = bf16[32,16,256]{2,1,0:T(8,128)(2,1)S(1)} collective-permute-done((bf16[32,16,256]{2,1,0:T(8,128)(2,1)S(1)}, bf16[32,16,256]{2,1,0:T(8,128)(2,1)S(1)}, u32[]{:S(2)}, u32[]{:S(2)}) %collective-permute-start.1) | collective-permute-done | bytes 262176 | tf_op jit(solution)/shard_map/ppermute | solution.py:153
  92.0 1.0 %fusion.1 = f32[32,16,256]{2,1,0:T(8,128)} fusion(bf16[32,16,256]{2,1,0:T(8,128)(2,1)S(1)} %collective-permute-done.1, f32[2,32,16,256]{3,2,1,0:T(8,128)S(1)} %convert_add_fusion, s32[]{:T(128)S(6)} %select_n.41), kind=kLoop, calls=%fused_computation.8 | loop fusion | flops 262144 | bytes 1310724 | tf_op jit(solution)/shard_map/sqrt | solution.py:155
  (17 shorter events, 0.1 us)
Async XLA Ops:
  0.6 1.2 %copy-start = (bf16[8,2,2,64,256]{4,3,2,1,0:T(8,128)(2,1)S(1)}, bf16[8,2,2,64,256]{4,3,2,1,0:T(8,128)(2,1)}, u32[]{:S(2)}) copy-start(bf16[8,2,2,64,256]{4,3,2,1,0:T(8,128)(2,1)} %param.11) | copy-start | bytes 3145732
  1.9 1.5 %copy-start.3 = (bf16[256,256,1]{1,0,2:T(8,128)(2,1)S(1)}, bf16[256,256,1]{1,0,2:T(8,128)(2,1)}, u32[]{:S(2)}) copy-start(bf16[256,256,1]{1,0,2:T(8,128)(2,1)} %constant.83) | copy-start | bytes 393220
  6.3 8.2 %copy-start.8 = (s32[8]{0:T(128)S(1)}, s32[8]{0:T(128)}, u32[]{:S(2)}) copy-start(s32[8]{0:T(128)} %param.17) | copy-start | bytes 100
  6.3 9.5 %copy-start.6 = (s32[8,8]{1,0:T(8,128)S(1)}, s32[8,8]{1,0:T(8,128)}, u32[]{:S(2)}) copy-start(s32[8,8]{1,0:T(8,128)} %param.13) | copy-start | bytes 772
  6.3 10.9 %copy-start.4 = (f32[8,2,256]{2,1,0:T(2,128)S(1)}, f32[8,2,256]{2,1,0:T(2,128)}, u32[]{:S(2)}) copy-start(f32[8,2,256]{2,1,0:T(2,128)} %param.12) | copy-start | bytes 49156
  6.3 10.9 %copy-start.5 = (s32[8,256]{1,0:T(8,128)S(1)}, s32[8,256]{1,0:T(8,128)}, u32[]{:S(2)}) copy-start(s32[8,256]{1,0:T(8,128)} %param.16) | copy-start | bytes 24580
  6.3 10.9 %copy-start.7 = (f32[129]{0:T(256)S(1)}, f32[129]{0:T(256)}, u32[]{:S(2)}) copy-start(f32[129]{0:T(256)} %param.15) | copy-start | bytes 1552
  6.3 49.5 %all-to-all-start = ((bf16[8,24,8,256]{3,2,1,0:T(8,128)(2,1)}), bf16[8,24,8,256]{3,2,1,0:T(8,128)(2,1)S(1)}, u32[]{:S(2)}, u32[]{:S(2)}) async-start(bf16[8,24,8,256]{3,2,1,0:T(8,128)(2,1)} %bitcast.36), calls=%async_computation | async-start | bytes 1572864 | tf_op jit(solution)/shard_map/all_to_all | solution.py:177
  55.8 8.5 %copy-start.1 = (bf16[8,24,8,256]{3,2,1,0:T(8,128)(2,1)}, bf16[8,24,8,256]{3,2,1,0:T(8,128)(2,1)S(1)}, u32[]{:S(2)}) copy-start(bf16[8,24,8,256]{3,2,1,0:T(8,128)(2,1)S(1)} %all-to-all-done.refs_0_) | copy-start | bytes 2359300
  55.8 17.2 %all-to-all-start.1 = ((bf16[8,12,8,256]{3,2,1,0:T(8,128)(2,1)}), bf16[8,12,8,256]{3,2,1,0:T(8,128)(2,1)S(1)}, u32[]{:S(2)}, u32[]{:S(2)}) async-start(bf16[8,12,8,256]{3,2,1,0:T(8,128)(2,1)} %bitcast.14), calls=%async_computation.1 | async-start | bytes 786432 | tf_op jit(solution)/shard_map/all_to_all | solution.py:178
  73.1 0.8 copy-start.2
  80.0 2.1 %collective-permute-start = (bf16[2,32,16,256]{3,2,1,0:T(8,128)(2,1)}, bf16[2,32,16,256]{3,2,1,0:T(8,128)(2,1)S(1)}, u32[]{:S(2)}, u32[]{:S(2)}) collective-permute-start(bf16[2,32,16,256]{3,2,1,0:T(8,128)(2,1)} %get-tuple-element.17), channel_id=1, source_target_pairs={{0,8},{8,0},{16,24},{24,16},{1,9},{9,1},{17,25},{25,17},{2,10},{10... | collective-permute-start | bytes 1572872 | tf_op jit(solution)/shard_map/ppermute | solution.py:148
  83.6 8.4 %collective-permute-start.1 = (bf16[32,16,256]{2,1,0:T(8,128)(2,1)S(1)}, bf16[32,16,256]{2,1,0:T(8,128)(2,1)S(1)}, u32[]{:S(2)}, u32[]{:S(2)}) collective-permute-start(bf16[32,16,256]{2,1,0:T(8,128)(2,1)S(1)} %fusion.2), channel_id=1, source_target_pairs={{0,16},{8,24},{16,0},{24,8},{1,17},{9,25},{17,1},{25,9},{2,18},{10... | collective-permute-start | bytes 786440 | tf_op jit(solution)/shard_map/ppermute | solution.py:153

commit v3 on v2

--- a/solution.py
+++ b/solution.py
@@ -167,33 +167,32 @@
     first = slab_rows - second
     edge = first + 2 * REACH
 
+    live_flag = (jnp.arange(slot_count, dtype=jnp.int32) < live_count[0]).astype(jnp.float32)
+    table_hit = dcf_index[:, :, None] == jnp.arange(dcf_table.shape[0], dtype=jnp.int32)[None, None, :]
+    density = jnp.sum(jnp.where(table_hit, dcf_table[None, None, :], 0.0), axis=2) * live_flag[:, None]
+
+    picked = slab_owner[:, None] * slab_rows + jnp.arange(block_len, dtype=jnp.int32)[None, :]
+    geometry = jnp.stack([coords[:, 0], coords[:, 1], density], axis=0)
+    geometry = jnp.pad(geometry, ((0, 0), (0, 0), (REACH, REACH)))
+    geometry = jnp.take(geometry, picked, axis=2, mode="clip")
+    starts = jnp.broadcast_to(
+        jnp.take(foot_offset, slab_owner, axis=1, mode="clip").astype(jnp.float32)[None, :, :, None],
+        (1, slot_count, slab_count, block_len),
+    )
+    geometry = jnp.transpose(jnp.concatenate([geometry, starts], axis=0), (2, 0, 3, 1))
+    got_geometry = lax.all_to_all(geometry, "spoke", split_axis=0, concat_axis=0, tiled=True)
+    geometry = jnp.transpose(got_geometry, (1, 2, 0, 3)).reshape(4, block_len * group)
+
     samples = kdata.reshape(slot_count, columns, grid_len)
     turned = sum(
         jnp.einsum("tcs,cd->std", samples, table, preferred_element_type=jnp.float32) for table in depth_tables
     ).astype(jnp.bfloat16)
     turned = jnp.pad(turned, ((REACH, REACH), (0, 0), (0, 0)))
-    picked = slab_owner[:, None] * slab_rows + jnp.arange(block_len, dtype=jnp.int32)[None, :]
     sent = [jnp.take(turned, part, axis=0, mode="clip") for part in (picked[:, :edge], picked[:, edge:])]
     got_first = lax.all_to_all(sent[0], "spoke", split_axis=0, concat_axis=0, tiled=True)
     got_second = lax.all_to_all(sent[1], "spoke", split_axis=0, concat_axis=0, tiled=True)
 
-    coords, dcf_index, _ = lax.optimization_barrier((coords, dcf_index, sent[0]))
-    live_flag = (jnp.arange(slot_count, dtype=jnp.int32) < live_count[0]).astype(jnp.float32)
-    table_hit = dcf_index[:, :, None] == jnp.arange(dcf_table.shape[0], dtype=jnp.int32)[None, None, :]
-    density = jnp.sum(jnp.where(table_hit, dcf_table[None, None, :], 0.0), axis=2) * live_flag[:, None]
-    starts = jnp.pad(foot_offset.astype(jnp.float32), ((0, 0), (0, grid_len - slab_count)))
-    geometry = jnp.stack([coords[:, 0], coords[:, 1], density, starts], axis=0)
-    geometry = lax.all_gather(geometry, "spoke", axis=1, tiled=True)
-
-    owned_slab = slab_owner[lax.axis_index("spoke")]
-    first_row = owned_slab * slab_rows
-    starts = lax.dynamic_slice(geometry, (3, 0, owned_slab), (1, group, 1))
-    near = lax.dynamic_slice_in_dim(
-        jnp.pad(geometry[:3], ((0, 0), (0, 0), (REACH, REACH))), first_row, block_len, axis=2
-    )
-    geometry = jnp.concatenate([near, jnp.broadcast_to(starts, (1, group, block_len))], axis=0)
-    geometry = jnp.transpose(geometry, (0, 2, 1)).reshape(4, block_len * group)
-
+    first_row = slab_owner[lax.axis_index("spoke")] * slab_rows
     core = lax.axis_index("coil") % 2
     place = jnp.stack([first_row, core]).astype(jnp.int32)
     shape = (slab_rows, coil_dev, part_count, kz_len, grid_len)

time: 93.5 us -> 83.6 us (0.89)
  blocking collectives: 38.2 us -> 0 us
  waiting for transfers between devices: 8.94 us -> 27.7 us
  local copies, waits for them, and re-layouts: 7.54 us -> 14.1 us
  starting transfers between devices: 12.5 us -> 15.9 us
  other arithmetic: 4.8 us -> 6.98 us
  between operations: 4.08 us -> 2.16 us
  matrix products: 2.06 us -> 1.12 us
    all_gather x1 -> x0, blocking collectives: 38.2 us -> none  [on_device(): geometry = lax.all_gather(geometry, 'spoke', axis=1, tiled=True)]
    all_to_all x1, waiting for transfers between devices: 0.01 us -> 16.1 us  [on_device(): lax.all_to_all(sent[0], 'spoke', split_axis=0, concat_axis=0, tiled=True)]
    all_to_all x0 -> x1, starting transfers between devices: none -> 7.28 us  [on_device(): lax.all_to_all(geometry, 'spoke', split_axis=0, concat_axis=0, tiled=True)]
    all_to_all x1, starting transfers between devices: 7.42 us -> 3.55 us  [on_device(): lax.all_to_all(sent[0], 'spoke', split_axis=0, concat_axis=0, tiled=True)]
    gather x0 -> x3, local copies, waits for them, and re-layouts: none -> 2.93 us  [the longest x2 2.37 us: on_device(): geometry = jnp.take(geometry, picked, axis=2, mode='clip')]
    all_to_all x0 -> x1, waiting for transfers between devices: none -> 2.71 us  [on_device(): lax.all_to_all(geometry, 'spoke', split_axis=0, concat_axis=0, tiled=True)]
    unnamed x19 -> x16, local copies, waits for them, and re-layouts: 1.73 us -> 3.43 us
    dot_general x2, matrix products: 2.06 us -> 1.12 us  [on_device(): jnp.einsum('tcs,cd->std', samples, table, preferred_element_type=jnp.floa...]
  transfers between devices with their start and end apart: 4 -> 5, of which waited for: 2 -> 4; matrix products, arithmetic and copies ran while one was open for 6% -> 12% of each run, Pallas kernels for 9% -> 11%
where the time goes in v3:
time: 83.6 us; the launch traced here: 82.9 us
  waiting for transfers between devices  27.7 us (33%)
  starting transfers between devices  15.9 us (19%)
  Pallas kernels  14.9 us (18%)
  local copies, waits for them, and re-layouts  14.1 us (17%)
  other arithmetic  6.98 us (8%)
  between operations  2.16 us (3%)
  matrix products  1.12 us (1%)
    all_to_all x1, waiting for transfers between devices, on_device(): lax.all_to_all(sent[0], 'spoke', split_axis=0, concat_axis=0, tiled=True)  16.1 us
    pallas_call x2, Pallas kernels, image_chunk(): pl.pallas_call(functools.partial(slab_kernel, group=group, value_count=le...  14.9 us
    all_to_all x1, starting transfers between devices, on_device(): lax.all_to_all(geometry, 'spoke', split_axis=0, concat_axis=0, tiled=True)  7.28 us
    ppermute x1, waiting for transfers between devices, coil_sum(): lax.ppermute(block, 'coil', [(i, (i + 2 * turn) % count) for i in range(c...  6.84 us
    all_to_all x1, starting transfers between devices, on_device(): lax.all_to_all(sent[0], 'spoke', split_axis=0, concat_axis=0, tiled=True)  3.55 us
    all_to_all x1, starting transfers between devices, on_device(): lax.all_to_all(sent[1], 'spoke', split_axis=0, concat_axis=0, tiled=True)  3.5 us
    unnamed x16, local copies, waits for them, and re-layouts  3.43 us
    gather x2, local copies, waits for them, and re-layouts, on_device(): jnp.take(turned, part, axis=0, mode='clip')  3.09 us
  transfers between devices with their start and end apart: 5, of which 4 were waited for; matrix products, arithmetic and copies ran while one was open for 12% of the time, Pallas kernels for 11%

profile of v3, /device:TPU:0, one launch (start us, length us, event | category | flops | bytes accessed | tf_op | source)
XLA Modules:
  0.0 82.9 jit_solution(4579745355966811672)
XLA Ops:
  0.6 0.7 broadcast_multiply_fusion
  1.4 0.7 pad_clamp_fusion.2
  2.7 0.1 iota_add_fusion.1
  2.8 0.1 reshape.91
  2.9 0.8 copy.48
  3.6 0.6 gather_fusion.1
  4.3 0.8 fusion.3
  5.1 0.9 %select_reduce_fusion = f32[8,256]{1,0:T(8,128)S(1)} fusion(f32[129]{0:T(256)} %param.15, s32[8,256]{1,0:T(8,128)} %param.16), kind=kLoop, calls=%fused_computation.6 | loop fusion | flops 790528 | bytes 16900 | tf_op jit(solution)/shard_map/reduce_sum | solution.py:172
  6.0 0.1 bitcast_multiply_fusion
  6.1 0.2 copy.46
  6.3 0.1 pad.8
  6.4 2.1 %gather_fusion = f32[288,3,8]{2,1,0:T(4,128)S(1)} fusion(f32[3,8,260]{1,0,2:T(4,128)S(1)} %pad.8, s32[1024]{0:T(1024)S(1)} %pad_clamp_fusion.3), kind=kCustom, calls=%fused_computation | custom fusion | bytes 56448 | tf_op jit(solution)/shard_map/jit(_take)/gather | solution.py:177
  8.6 0.2 copy.58
  8.8 0.1 broadcast_in_dim.41
  9.0 0.8 reshape.129
  9.7 7.3 %all-to-all-start = ((f32[8,1,1152]{2,1,0:T(1,128)}), f32[8,1,1152]{2,1,0:T(1,128)S(1)}, u32[]{:S(2)}, u32[]{:S(2)}) async-start(f32[8,1,1152]{2,1,0:T(1,128)} %reshape.129), calls=%async_computation | async-start | bytes 73728 | tf_op jit(solution)/shard_map/all_to_all | solution.py:183
  17.1 0.1 reshape.107
  17.2 0.6 fusion.4
  17.8 0.3 copy-done.3
  18.1 0.6 fusion
  18.7 0.6 copy.61
  19.2 0.1 pad.9.clone
  19.3 1.7 %gather_fusion.2 = bf16[192,8,256]{2,1,0:T(8,128)(2,1)} fusion(bf16[260,8,256]{2,1,0:T(8,128)(2,1)S(1)} %pad.9.clone, s32[1024]{0:T(1024)S(1)} %pad_clamp_fusion.1), kind=kCustom, calls=%fused_computation.2 | custom fusion | bytes 1573632 | tf_op jit(solution)/shard_map/jit(_take)/gather | solution.py:191
  21.0 2.7 %all-to-all-done = f32[8,1,1152]{2,1,0:T(1,128)S(1)} async-done(((f32[8,1,1152]{2,1,0:T(1,128)}), f32[8,1,1152]{2,1,0:T(1,128)S(1)}, u32[]{:S(2)}, u32[]{:S(2)}) %all-to-all-start) | async-done | bytes 36896 | tf_op jit(solution)/shard_map/all_to_all | solution.py:183
  23.7 3.5 %all-to-all-start.1 = ((bf16[8,24,8,256]{3,2,1,0:T(8,128)(2,1)}), bf16[8,24,8,256]{3,2,1,0:T(8,128)(2,1)S(1)}, u32[]{:S(2)}, u32[]{:S(2)}) async-start(bf16[8,24,8,256]{3,2,1,0:T(8,128)(2,1)} %bitcast.46), calls=%async_computation.1 | async-start | bytes 1572864 | tf_op jit(solution)/shard_map/all_to_all | solution.py:192
  27.3 0.1 slice.22
  27.4 0.6 dynamic_slice.10
  28.0 0.1 reshape.115
  28.0 1.4 %gather_fusion.3 = bf16[96,8,256]{2,1,0:T(8,128)(2,1)} fusion(bf16[260,8,256]{2,1,0:T(8,128)(2,1)S(1)} %pad.9.clone, s32[1024]{0:T(1024)S(1)} %pad_clamp_fusion), kind=kCustom, calls=%fused_computation.3 | custom fusion | bytes 786816 | tf_op jit(solution)/shard_map/jit(_take)/gather | solution.py:191
  30.1 0.7 pad_add_fusion.1.place_ref
  30.8 16.1 %all-to-all-done.1.refs_0_ = bf16[8,24,8,256]{3,2,1,0:T(8,128)(2,1)S(1)} async-done(((bf16[8,24,8,256]{3,2,1,0:T(8,128)(2,1)}), bf16[8,24,8,256]{3,2,1,0:T(8,128)(2,1)S(1)}, u32[]{:S(2)}, u32[]{:S(2)}) %all-to-all-start.1) | async-done | bytes 786464 | tf_op jit(solution)/shard_map/all_to_all | solution.py:192
  46.8 3.5 %all-to-all-start.2 = ((bf16[8,12,8,256]{3,2,1,0:T(8,128)(2,1)}), bf16[8,12,8,256]{3,2,1,0:T(8,128)(2,1)S(1)}, u32[]{:S(2)}, u32[]{:S(2)}) async-start(bf16[8,12,8,256]{3,2,1,0:T(8,128)(2,1)} %bitcast.15), calls=%async_computation.2 | async-start | bytes 786432 | tf_op jit(solution)/shard_map/all_to_all | solution.py:193
  50.3 0.6 pad_add_fusion.place_ref
  51.0 0.5 broadcast.76
  51.5 0.7 reduce
  52.2 0.2 reshape.130
  52.4 0.3 copy.51
  52.7 0.3 reshape.87
  53.1 0.6 slice.32.geometry_ref
  53.7 0.6 slice.33.geometry_ref
  54.3 8.7 %shard_map.122 = (f32[32,2,2,64,256]{4,3,2,1,0:T(8,128)}, f32[2,32,16,256]{3,2,1,0:T(8,128)}, bf16[2,32,16,256]{3,2,1,0:T(8,128)(2,1)}) custom-call(s32[2]{0:T(128)} %pad_add_fusion.1.place_ref, f32[4,1536]{1,0:T(4,128)} %slice.33.geometry_ref, bf16[512,512]{1,0:T(8,128)(2,1)} %constant.69.clone.high_ref, bf16[512,512]{1,0:T(8,128)(2,1)} %constant.70.clone.low_ref, ...), custom_call_target="tpu_custom_call" | custom-call | flops 3690987520 | bytes 5242880 | tf_op jit(solution)/shard_map/pallas_call | solution.py:110
  63.0 0.8 copy-done.2
  63.8 6.2 %shard_map.123 = (f32[32,2,2,64,256]{4,3,2,1,0:T(8,128)}, f32[2,32,16,256]{3,2,1,0:T(8,128)}, bf16[2,32,16,256]{3,2,1,0:T(8,128)(2,1)}) custom-call(s32[2]{0:T(128)} %pad_add_fusion.place_ref, f32[4,1024]{1,0:T(4,128)} %slice.32.geometry_ref, bf16[512,512]{1,0:T(8,128)(2,1)} %constant.69.clone.high_ref, ...), custom_call_target="tpu_custom_call", output_to_operand_aliasing={{0}: (6, {}), {1}: (7, {}), {2}: (8, {})} | custom-call | flops 2214592512 | bytes 3145728 | tf_op jit(solution)/shard_map/pallas_call | solution.py:110
  70.0 2.1 %collective-permute-done = bf16[2,32,16,256]{3,2,1,0:T(8,128)(2,1)S(1)} collective-permute-done((bf16[2,32,16,256]{3,2,1,0:T(8,128)(2,1)}, bf16[2,32,16,256]{3,2,1,0:T(8,128)(2,1)S(1)}, u32[]{:S(2)}, u32[]{:S(2)}) %collective-permute-start) | collective-permute-done | bytes 524320 | tf_op jit(solution)/shard_map/ppermute | solution.py:148
  72.1 1.4 %convert_add_fusion = f32[2,32,16,256]{3,2,1,0:T(8,128)S(1)} fusion(f32[2,32,16,256]{3,2,1,0:T(8,128)} %get-tuple-element.12, bf16[2,32,16,256]{3,2,1,0:T(8,128)(2,1)S(1)} %collective-permute-done), kind=kLoop, calls=%fused_computation.8 | loop fusion | flops 524288 | bytes 2621440 | tf_op jit(solution)/shard_map/add | solution.py:149
  73.5 1.6 %collective-permute-start.1 = (bf16[32,16,256]{2,1,0:T(8,128)(2,1)S(1)}, bf16[32,16,256]{2,1,0:T(8,128)(2,1)S(1)}, u32[]{:S(2)}, u32[]{:S(2)}) collective-permute-start(bf16[32,16,256]{2,1,0:T(8,128)(2,1)S(1)} %fusion.2), channel_id=1, source_target_pairs={{0,16},{8,24},{16,0},{24,8},{1,17},{9,25},{17,1},{25,9},{2,18},{10... | collective-permute-start | bytes 786440 | tf_op jit(solution)/shard_map/ppermute | solution.py:153
  75.1 6.8 %collective-permute-done.1 = bf16[32,16,256]{2,1,0:T(8,128)(2,1)S(1)} collective-permute-done((bf16[32,16,256]{2,1,0:T(8,128)(2,1)S(1)}, bf16[32,16,256]{2,1,0:T(8,128)(2,1)S(1)}, u32[]{:S(2)}, u32[]{:S(2)}) %collective-permute-start.1) | collective-permute-done | bytes 262176 | tf_op jit(solution)/shard_map/ppermute | solution.py:153
  82.0 1.0 %fusion.1 = f32[32,16,256]{2,1,0:T(8,128)} fusion(bf16[32,16,256]{2,1,0:T(8,128)(2,1)S(1)} %collective-permute-done.1, f32[2,32,16,256]{3,2,1,0:T(8,128)S(1)} %convert_add_fusion, s32[]{:T(128)S(6)} %select_n.33), kind=kLoop, calls=%fused_computation.10 | loop fusion | flops 262144 | bytes 1310724 | tf_op jit(solution)/shard_map/sqrt | solution.py:155
  (25 shorter events, 0.3 us)
Async XLA Ops:
  0.6 16.5 %copy-start = (bf16[8,2,2,64,256]{4,3,2,1,0:T(8,128)(2,1)S(1)}, bf16[8,2,2,64,256]{4,3,2,1,0:T(8,128)(2,1)}, u32[]{:S(2)}) copy-start(bf16[8,2,2,64,256]{4,3,2,1,0:T(8,128)(2,1)} %param.11) | copy-start | bytes 3145732
  6.4 10.7 %copy-start.4 = (bf16[256,256,1]{1,0,2:T(8,128)(2,1)S(1)}, bf16[256,256,1]{1,0,2:T(8,128)(2,1)}, u32[]{:S(2)}) copy-start(bf16[256,256,1]{1,0,2:T(8,128)(2,1)} %constant.77) | copy-start | bytes 393220
  9.7 14.0 %all-to-all-start = ((f32[8,1,1152]{2,1,0:T(1,128)}), f32[8,1,1152]{2,1,0:T(1,128)S(1)}, u32[]{:S(2)}, u32[]{:S(2)}) async-start(f32[8,1,1152]{2,1,0:T(1,128)} %reshape.129), calls=%async_computation | async-start | bytes 73728 | tf_op jit(solution)/shard_map/all_to_all | solution.py:183
  17.2 0.9 %copy-start.3 = (bf16[256,256,1]{1,0,2:T(8,128)(2,1)S(1)}, bf16[256,256,1]{1,0,2:T(8,128)(2,1)}, u32[]{:S(2)}) copy-start(bf16[256,256,1]{1,0,2:T(8,128)(2,1)} %constant.78) | copy-start | bytes 393220
  21.0 6.3 %copy-start.5 = (s32[8]{0:T(128)S(1)}, s32[8]{0:T(128)}, u32[]{:S(2)}) copy-start(s32[8]{0:T(128)} %param.17) | copy-start | bytes 100
  23.7 23.1 %all-to-all-start.1 = ((bf16[8,24,8,256]{3,2,1,0:T(8,128)(2,1)}), bf16[8,24,8,256]{3,2,1,0:T(8,128)(2,1)S(1)}, u32[]{:S(2)}, u32[]{:S(2)}) async-start(bf16[8,24,8,256]{3,2,1,0:T(8,128)(2,1)} %bitcast.46), calls=%async_computation.1 | async-start | bytes 1572864 | tf_op jit(solution)/shard_map/all_to_all | solution.py:192
  46.8 6.2 %copy-start.1 = (bf16[8,24,8,256]{3,2,1,0:T(8,128)(2,1)}, bf16[8,24,8,256]{3,2,1,0:T(8,128)(2,1)S(1)}, u32[]{:S(2)}) copy-start(bf16[8,24,8,256]{3,2,1,0:T(8,128)(2,1)S(1)} %all-to-all-done.1.refs_0_) | copy-start | bytes 2359300
  46.8 16.2 %all-to-all-start.2 = ((bf16[8,12,8,256]{3,2,1,0:T(8,128)(2,1)}), bf16[8,12,8,256]{3,2,1,0:T(8,128)(2,1)S(1)}, u32[]{:S(2)}, u32[]{:S(2)}) async-start(bf16[8,12,8,256]{3,2,1,0:T(8,128)(2,1)} %bitcast.15), calls=%async_computation.2 | async-start | bytes 786432 | tf_op jit(solution)/shard_map/all_to_all | solution.py:193
  63.0 0.8 copy-start.2
  70.0 2.1 %collective-permute-start = (bf16[2,32,16,256]{3,2,1,0:T(8,128)(2,1)}, bf16[2,32,16,256]{3,2,1,0:T(8,128)(2,1)S(1)}, u32[]{:S(2)}, u32[]{:S(2)}) collective-permute-start(bf16[2,32,16,256]{3,2,1,0:T(8,128)(2,1)} %get-tuple-element.13), channel_id=1, source_target_pairs={{0,8},{8,0},{16,24},{24,16},{1,9},{9,1},{17,25},{25,17},{2,10},{10... | collective-permute-start | bytes 1572872 | tf_op jit(solution)/shard_map/ppermute | solution.py:148
  73.5 8.4 %collective-permute-start.1 = (bf16[32,16,256]{2,1,0:T(8,128)(2,1)S(1)}, bf16[32,16,256]{2,1,0:T(8,128)(2,1)S(1)}, u32[]{:S(2)}, u32[]{:S(2)}) collective-permute-start(bf16[32,16,256]{2,1,0:T(8,128)(2,1)S(1)} %fusion.2), channel_id=1, source_target_pairs={{0,16},{8,24},{16,0},{24,8},{1,17},{9,25},{17,1},{25,9},{2,18},{10... | collective-permute-start | bytes 786440 | tf_op jit(solution)/shard_map/ppermute | solution.py:153
